TPU v7x, 64 devices: a 2x2x8 block of a 4x4x8 slice. The times are simulated.
64 devices in a mesh: dp: 4 (over x, y), tp: 16 (over z, core).
Axes of the slice: x: 2, y: 2, z: 8, core: 2. Of those that a mesh axis runs over, the one named last changes fastest.
The devices are a block of a 4x4x8 slice.
Arguments:
- x_in: bfloat16 [8192, 2048], P('dp'), parts along dimension 0
- h_mid: bfloat16 [8192, 2048], P('dp'), parts along dimension 0
- mean_x: float32 [8192], P('dp'), parts along dimension 0
- rstd_x: float32 [8192], P('dp'), parts along dimension 0
- mean_h: float32 [8192], P('dp'), parts along dimension 0
- rstd_h: float32 [8192], P('dp'), parts along dimension 0
- gain_x: bfloat16 [2048], replicated
- gain_h: bfloat16 [2048], replicated
- w_qkv: bfloat16 [2048, 6144], P(None, 'tp')
- w_out: bfloat16 [16, 128, 2048], P('tp')
- w_gate: bfloat16 [2048, 8192], P(None, 'tp')
- w_up: bfloat16 [2048, 8192], P(None, 'tp')
- w_down: bfloat16 [8192, 2048], P('tp')
- d_out: bfloat16 [8192, 2048], P('dp'), parts along dimension 0
Outputs:
- output 1: bfloat16 [8192, 2048], P('dp'), parts along dimension 0
- output 2: bfloat16 [8192, 6144], P('dp', 'tp'), parts along dimension 0
- output 3: bfloat16 [64, 128, 2048], P(('dp', 'tp')), parts along dimension 0
- output 4: bfloat16 [8192, 8192], P('dp', 'tp'), parts along dimension 0
- output 5: bfloat16 [8192, 8192], P('dp', 'tp'), parts along dimension 0
- output 6: bfloat16 [32768, 2048], P(('dp', 'tp')), parts along dimension 0
There are 4 independent parts. A program takes and returns all parts, laid end to end along the dimension named above; an argument that names none is the same for every part.
All inputs are finite; a program needn't handle non-finite values.
Results may differ from a plain program's by a relative error of at most 0.0180282.
Values are sent between devices in bfloat16 or wider.
A program may use at most 768 MiB of HBM per device.

v0:
```python
import jax
import jax.numpy as jnp
from jax import lax
from jax.sharding import PartitionSpec as P


def layer_norm(src_rows, row_mean, row_rstd, gain_vec):
    centred = (src_rows.astype(jnp.float32) - row_mean[..., None]) * row_rstd[..., None]
    return (centred * gain_vec.astype(jnp.float32)).astype(jnp.bfloat16)


def norm_backward(grad_n, src_rows, row_mean, row_rstd, gain_vec):
    centred = (src_rows.astype(jnp.float32) - row_mean[..., None]) * row_rstd[..., None]
    scaled = grad_n * gain_vec.astype(jnp.float32)
    mean_grad = jnp.mean(scaled, axis=-1, keepdims=True)
    mean_proj = jnp.mean(scaled * centred, axis=-1, keepdims=True)
    return row_rstd[..., None] * (scaled - mean_grad - centred * mean_proj)


def local_attention(qkv_rows, d_heads):
    group_size = qkv_rows.shape[2] - 2
    queries = qkv_rows[:, :, :group_size]
    key_rows = qkv_rows[:, :, group_size]
    value_rows = qkv_rows[:, :, group_size + 1]
    score_scale = qkv_rows.shape[3] ** -0.5
    positions = jnp.arange(qkv_rows.shape[0])
    causal = positions[:, None] >= positions[None, :]
    scores = jnp.einsum('tkgd,skd->kgts', queries, key_rows, preferred_element_type=jnp.float32) * score_scale
    attn_probs = jax.nn.softmax(jnp.where(causal, scores, -1e30), axis=-1)
    probs_low = attn_probs.astype(jnp.bfloat16)
    outputs = jnp.einsum('kgts,skd->tkgd', probs_low, value_rows, preferred_element_type=jnp.float32).astype(jnp.bfloat16)
    d_probs = jnp.einsum('tkgd,skd->kgts', d_heads, value_rows, preferred_element_type=jnp.float32)
    row_dot = jnp.sum(attn_probs * d_probs, axis=-1, keepdims=True)
    d_scores = (attn_probs * (d_probs - row_dot) * score_scale).astype(jnp.bfloat16)
    grad_q = jnp.einsum('kgts,skd->tkgd', d_scores, key_rows, preferred_element_type=jnp.float32)
    grad_k = jnp.einsum('kgts,tkgd->skd', d_scores, queries, preferred_element_type=jnp.float32)
    grad_v = jnp.einsum('kgts,tkgd->skd', probs_low, d_heads, preferred_element_type=jnp.float32)
    d_qkv = jnp.concatenate([grad_q, grad_k[:, :, None], grad_v[:, :, None]], axis=2)
    return outputs, d_qkv.astype(jnp.bfloat16)


def solution(mesh):
    def device_step(x_in, h_mid, mean_x, rstd_x, mean_h, rstd_h, gain_x, gain_h, w_qkv, w_out, w_gate, w_up, w_down, d_out):
        heads_local, head_dim = w_out.shape[0], w_out.shape[1]
        kv_local = (w_qkv.shape[1] // head_dim - heads_local) // 2
        group_size = heads_local // kv_local
        tokens = x_in.shape[0]
        norm_h = layer_norm(h_mid, mean_h, rstd_h, gain_h)
        gate_f = jnp.dot(norm_h, w_gate, preferred_element_type=jnp.float32).astype(jnp.bfloat16).astype(jnp.float32)
        up_f = jnp.dot(norm_h, w_up, preferred_element_type=jnp.float32).astype(jnp.bfloat16).astype(jnp.float32)
        sig_gate = jax.nn.sigmoid(gate_f)
        gate_act = gate_f * sig_gate
        hidden = (gate_act * up_f).astype(jnp.bfloat16)
        d_w_down = jnp.einsum('tf,te->fe', hidden, d_out, preferred_element_type=jnp.float32).astype(jnp.bfloat16)
        d_hidden = jnp.einsum('te,fe->tf', d_out, w_down, preferred_element_type=jnp.float32).astype(jnp.bfloat16).astype(jnp.float32)
        d_gate = (d_hidden * up_f * sig_gate * (1.0 + gate_f * (1.0 - sig_gate))).astype(jnp.bfloat16)
        d_up = (d_hidden * gate_act).astype(jnp.bfloat16)
        d_w_gate = jnp.einsum('td,tf->df', norm_h, d_gate, preferred_element_type=jnp.float32).astype(jnp.bfloat16)
        d_w_up = jnp.einsum('td,tf->df', norm_h, d_up, preferred_element_type=jnp.float32).astype(jnp.bfloat16)
        part_h = jnp.einsum('tf,df->td', d_gate, w_gate, preferred_element_type=jnp.float32) + jnp.einsum('tf,df->td', d_up, w_up, preferred_element_type=jnp.float32)
        d_norm_h = lax.psum(part_h.astype(jnp.bfloat16), 'tp').astype(jnp.float32)
        d_mid = d_out.astype(jnp.float32) + norm_backward(d_norm_h, h_mid, mean_h, rstd_h, gain_h)
        d_mid_b = d_mid.astype(jnp.bfloat16)
        norm_x = layer_norm(x_in, mean_x, rstd_x, gain_x)
        qkv_rows = jnp.dot(norm_x, w_qkv, preferred_element_type=jnp.float32).astype(jnp.bfloat16)
        qkv_rows = qkv_rows.reshape(tokens, kv_local, group_size + 2, head_dim)
        d_heads = jnp.einsum('te,hze->thz', d_mid_b, w_out, preferred_element_type=jnp.float32).astype(jnp.bfloat16)
        outputs, d_qkv = local_attention(qkv_rows, d_heads.reshape(tokens, kv_local, group_size, head_dim))
        d_w_out = jnp.einsum('thz,te->hze', outputs.reshape(tokens, heads_local, head_dim), d_mid_b, preferred_element_type=jnp.float32).astype(jnp.bfloat16)
        d_qkv = d_qkv.reshape(tokens, w_qkv.shape[1])
        d_w_qkv = jnp.einsum('td,tc->dc', norm_x, d_qkv, preferred_element_type=jnp.float32).astype(jnp.bfloat16)
        part_x = jnp.einsum('tc,dc->td', d_qkv, w_qkv, preferred_element_type=jnp.float32)
        d_norm_x = lax.psum(part_x.astype(jnp.bfloat16), 'tp').astype(jnp.float32)
        d_x = (d_mid + norm_backward(d_norm_x, x_in, mean_x, rstd_x, gain_x)).astype(jnp.bfloat16)
        return d_x, d_w_qkv, d_w_out, d_w_gate, d_w_up, d_w_down

    row_spec = P('dp', None)
    stat_spec = P('dp')
    col_spec = P(None, 'tp')
    in_specs = (row_spec, row_spec, stat_spec, stat_spec, stat_spec, stat_spec, P(None), P(None), col_spec, P('tp', None, None), col_spec, col_spec, P('tp', None), row_spec)
    out_specs = (row_spec, P('dp', 'tp'), P(('dp', 'tp'), None, None), P('dp', 'tp'), P('dp', 'tp'), P(('dp', 'tp'), None))
    return jax.shard_map(device_step, mesh=mesh, in_specs=in_specs, out_specs=out_specs, check_vma=False)
```

profile of v0, /device:TPU:21, one launch (start us, length us, event | category | flops | bytes accessed | tf_op | source)
XLA Modules:
  0.0 416.9 jit_solution(6471052565666892079)
XLA Ops:
  8.1 5.5 %multiply_convert_fusion.1 = bf16[2048,2048]{1,0:T(8,128)(2,1)S(1)} fusion(bf16[2048,2048]{1,0:T(8,128)(2,1)} %param.15, f32[2048]{0:T(1024)S(1)} %convert_element_type.121, f32[2048]{0:T(1024)} %param.18, f32[2048]{0:T(1024)} %param.19), kind=kLoop, calls=%fused_computation.20 | loop fusion | flops 20971520 | bytes 16801792 | tf_op jit(solution)/shard_map/convert_element_type | solution.py:9
  13.7 4.7 %convolution_convert_fusion.4 = bf16[2048,512]{1,0:T(8,128)(2,1)S(1)} fusion(bf16[2048,2048]{1,0:T(8,128)(2,1)S(1)} %multiply_convert_fusion.1, bf16[2048,512]{1,0:T(8,128)(2,1)S(1)} %copy-done), kind=kOutput, calls=%fused_computation.54 | convolution fusion | flops 4296015872 | bytes 12582912 | tf_op jit(solution)/shard_map/dot_general | solution.py:49
  18.4 4.7 %convolution_convert_fusion.5 = bf16[2048,512]{1,0:T(8,128)(2,1)S(1)} fusion(bf16[2048,2048]{1,0:T(8,128)(2,1)S(1)} %multiply_convert_fusion.1, bf16[2048,512]{1,0:T(8,128)(2,1)S(1)} %copy-done.22), kind=kOutput, calls=%fused_computation.55 | convolution fusion | flops 4296015872 | bytes 12582912 | tf_op jit(solution)/shard_map/dot_general | solution.py:50
  23.2 5.0 %convolution_convert_fusion.6 = bf16[2048,512]{1,0:T(8,128)(2,1)S(1)} fusion(bf16[2048,2048]{1,0:T(8,128)(2,1)S(1)} %bitcast.129, bf16[512,2048]{1,0:T(8,128)(2,1)S(1)} %copy-done.21), kind=kOutput, calls=%fused_computation.56 | convolution fusion | flops 4296015872 | bytes 12582912 | tf_op jit(solution)/shard_map/te,fe->tf/dot_general | solution.py:55
  28.2 1.3 copy-done.27
  29.5 10.2 %fusion.70 = f32[2048,2048]{1,0:T(8,128)} fusion(bf16[2048,512]{1,0:T(8,128)(2,1)S(1)} %copy-done, bf16[2048,512]{1,0:T(8,128)(2,1)S(1)} %convolution_convert_fusion.5, bf16[2048,512]{1,0:T(8,128)(2,1)S(1)} %convolution_convert_fusion.6, bf16[2048,512]{1,0:T(8,128)(2,1)S(1)} %convolution_convert_fusion.4), kind=kOutput, calls=%fused_computation.86 | convolution fusion | flops 4308598784 | bytes 25165824 | tf_op jit(solution)/shard_map/tf,df->td/dot_general | solution.py:60
  39.7 16.1 %add_convert_fusion.1 = bf16[2048,2048]{1,0:T(8,128)(2,1)} fusion(f32[2048,2048]{1,0:T(8,128)} %fusion.70, bf16[2048,512]{1,0:T(8,128)(2,1)} %param.25, bf16[2048,512]{1,0:T(8,128)(2,1)} %copy-done.27, bf16[2048,512]{1,0:T(8,128)(2,1)} %copy-done.25), kind=kOutput, calls=%fused_computation.19 | convolution fusion | flops 4311744512 | bytes 31457280 | tf_op jit(solution)/shard_map/tf,df->td/dot_general | solution.py:60
  56.6 5.6 %multiply_convert_fusion = bf16[2048,2048]{1,0:T(8,128)(2,1)S(1)} fusion(bf16[2048,2048]{1,0:T(8,128)(2,1)} %param.14, f32[2048]{0:T(1024)S(1)} %convert_element_type.132, f32[2048]{0:T(1024)S(1)} %copy-done.16, f32[2048]{0:T(1024)S(1)} %copy-done.18), kind=kLoop, calls=%fused_computation.13 | loop fusion | flops 20971520 | bytes 16801792 | tf_op jit(solution)/shard_map/convert_element_type | solution.py:9
  62.2 3.7 convolution_convert_fusion.8
  66.4 2.4 fusion.8
  68.9 5.7 %copy-done.3 = f32[2048,2048]{1,0:T(8,128)} copy-done((f32[2048,2048]{1,0:T(8,128)}, f32[2048,2048]{1,0:T(8,128)S(1)}, u32[]{:S(2)}) %copy-start.3) | copy-done | bytes 16777240
  74.6 4.7 %fusion.7 = f32[2048]{0:T(1024)S(1)} fusion(f32[2048,2048]{1,0:T(8,128)S(1)} %get-tuple-element.11, f32[2048]{0:T(1024)S(1)} %get-tuple-element.10), kind=kLoop, calls=%fused_computation.23 | loop fusion | flops 20969472 | bytes 16793600 | tf_op jit(solution)/shard_map/reduce_sum | solution.py:29
  79.3 6.9 %convolution_convert_fusion.3 = bf16[2048,512]{1,0:T(8,128)(2,1)} fusion(bf16[2048,2048]{1,0:T(8,128)(2,1)S(1)} %bitcast.131, bf16[2048,512]{1,0:T(8,128)(2,1)S(1)} %copy-done.30, bf16[2048,512]{1,0:T(8,128)(2,1)S(1)} %copy-done.28, bf16[2048,512]{1,0:T(8,128)(2,1)S(1)} %copy-done.26), kind=kOutput, calls=%fused_computation.53 | convolution fusion | flops 4309647360 | bytes 16777216 | tf_op jit(solution)/shard_map/td,tf->df/dot_general | solution.py:58
  86.2 7.1 %convolution_convert_fusion.2 = bf16[2048,512]{1,0:T(8,128)(2,1)} fusion(bf16[2048,2048]{1,0:T(8,128)(2,1)S(1)} %bitcast.131, bf16[2048,512]{1,0:T(8,128)(2,1)S(1)} %copy-done.28, bf16[2048,512]{1,0:T(8,128)(2,1)S(1)} %copy-done.26), kind=kOutput, calls=%fused_computation.52 | convolution fusion | flops 4304404480 | bytes 14680064 | tf_op jit(solution)/shard_map/td,tf->df/dot_general | solution.py:59
  93.3 94.3 %all-reduce.3.cloned.1.call-done = bf16[2048,2048]{1,0:T(8,128)(2,1)} async-done(((bf16[2048,2048]{1,0:T(8,128)(2,1)}), bf16[2048,2048]{1,0:T(8,128)(2,1)}) %all-reduce.3.cloned.1.call-update) | async-done | bytes 8388624 | tf_op jit(solution)/shard_map/psum | solution.py:61
  187.6 9.2 %fusion.5 = (f32[2048]{0:T(1024)S(1)}, f32[2048]{0:T(1024)S(1)}) fusion(bf16[2048,2048]{1,0:T(8,128)(2,1)} %all-reduce.3.cloned.1.call-done, f32[2048]{0:T(1024)S(1)} %convert_element_type.121, f32[2048]{0:T(1024)S(1)} %copy-done.15, f32[2048]{0:T(1024)S(1)} %copy-done.14, bf16[2048,2048]{1,0:T(8,128)(2,1)} %param.15), kind=kLoop, calls=%fused_computation.18 | loop fusion | flops 33550336 | bytes 16818176 | tf_op jit(solution)/shard_map/reduce_sum | solution.py:15
  196.8 10.3 %multiply_add_fusion = f32[2048,2048]{1,0:T(8,128)S(1)} fusion(bf16[2048,2048]{1,0:T(8,128)(2,1)S(1)} %copy-done.4, bf16[2048,2048]{1,0:T(8,128)(2,1)} %param.15, bf16[2048,2048]{1,0:T(8,128)(2,1)} %param.27, f32[2048]{0:T(1024)S(1)} %get-tuple-element.14, f32[2048]{0:T(1024)S(1)} %get-tuple-element.15, f32[2048]{0:T(1024)S(1)} %convert_element_type.121, ...), kind=kLoop, calls=%fused_computation.15 | loop fusion | flops 46137344 | bytes 41984000 | tf_op jit(solution)/shard_map/add | solution.py:62
  207.2 2.4 fusion.34
  209.6 3.3 copy-done.2
  212.9 9.4 %fusion.48 = bf16[2048,1,1,128]{0,3,2,1:T(8,128)(2,1)S(1)} fusion(bf16[2048,128]{1,0:T(8,128)(2,1)S(1)} %fusion.34, f32[2048]{0:T(1024)S(1)} %fusion.7, f32[2048]{0:T(1024)S(1)} %get-tuple-element.10, f32[2048,2048]{1,0:T(8,128)} %copy-done.3), kind=kOutput, calls=%fused_computation.69 | convolution fusion | flops 1099169792 | bytes 17842176 | tf_op jit(solution)/shard_map/kgts,tkgd->skd/dot_general | solution.py:37
  222.3 12.8 %fusion = (f32[2048]{0:T(1024)S(1)}, f32[2048,2048]{1,0:T(8,128)}) fusion(f32[2048]{0:T(1024)S(1)} %fusion.7, f32[2048]{0:T(1024)S(1)} %get-tuple-element.10, f32[2048,2048]{1,0:T(8,128)} %copy-done.3, bf16[2048,128]{1,0:T(8,128)(2,1)S(1)} %fusion.34, bf16[2048,1,3,128]{0,3,2,1:T(8,128)(2,1)S(1)} %bitcast.135), kind=kOutput, calls=%fused_computation.3 | convolution fusion | flops 1103099904 | bytes 34627584 | tf_op jit(solution)/shard_map/tkgd,skd->kgts/dot_general | solution.py:32
  235.1 9.5 %fusion.9 = bf16[2048,2048]{0,1:T(8,128)(2,1)S(1)} fusion(f32[2048,2048]{1,0:T(8,128)} %get-tuple-element.13, f32[2048]{0:T(1024)S(1)} %get-tuple-element.12, f32[2048]{0:T(1024)S(1)} %fusion.7, f32[2048]{0:T(1024)S(1)} %get-tuple-element.10, f32[2048,2048]{1,0:T(8,128)S(1)} %bitcast.127), kind=kLoop, calls=%fused_computation.25 | loop fusion | flops 37748736 | bytes 41967616 | tf_op jit(solution)/shard_map/reshape.22
  244.7 2.9 fusion.44
  247.6 2.5 fusion.43
  250.3 1.1 copy-done.8
  251.4 7.0 %convolution_convert_fusion = bf16[2048,2048]{1,0:T(8,128)(2,1)} fusion(bf16[2048,384]{0,1:T(8,128)(2,1)S(1)} %bitcast.132, bf16[2048,384]{1,0:T(8,128)(2,1)S(1)} %copy-done.24), kind=kOutput, calls=%fused_computation.31 | convolution fusion | flops 3225419776 | bytes 11534336 | tf_op jit(solution)/shard_map/tc,dc->td/dot_general | solution.py:72
  258.5 11.2 %convolution_convert_fusion.1 = bf16[512,2048]{1,0:T(8,128)(2,1)} fusion(bf16[2048,2048]{1,0:T(8,128)(2,1)} %param.27, bf16[2048,512]{1,0:T(8,128)(2,1)} %copy-done.29, bf16[2048,512]{1,0:T(8,128)(2,1)} %copy-done.25), kind=kOutput, calls=%fused_computation.51 | convolution fusion | flops 4304404480 | bytes 14680064 | tf_op jit(solution)/shard_map/tf,te->fe/dot_general | solution.py:54
  269.7 9.1 %convolution_convert_fusion.7 = bf16[2048,384]{1,0:T(8,128)(2,1)} fusion(bf16[2048,2048]{1,0:T(8,128)(2,1)} %copy-done.6, bf16[2048,384]{0,1:T(8,128)(2,1)S(1)} %bitcast.133), kind=kOutput, calls=%fused_computation.57 | convolution fusion | flops 3222011904 | bytes 11534336 | tf_op jit(solution)/shard_map/td,tc->dc/dot_general | solution.py:71
  278.8 15.2 %fusion.40 = bf16[1,128,2048]{2,1,0:T(8,128)(2,1)} fusion(f32[2048,2048]{1,0:T(8,128)} %copy-done.2, bf16[2048,1,3,128]{0,3,2,1:T(8,128)(2,1)} %bitcast.138, f32[2048]{0:T(1024)S(1)} %fusion.7, f32[2048]{0:T(1024)S(1)} %get-tuple-element.10, f32[2048,2048]{1,0:T(8,128)} %copy-done.3), kind=kOutput, calls=%fused_computation.65 | convolution fusion | flops 2177368064 | bytes 34619392 | tf_op jit(solution)/shard_map/thz,te->hze/dot_general | solution.py:69
  294.0 92.6 %all-reduce.5.cloned.1.call-done = bf16[2048,2048]{1,0:T(8,128)(2,1)} async-done(((bf16[2048,2048]{1,0:T(8,128)(2,1)}), bf16[2048,2048]{1,0:T(8,128)(2,1)}) %all-reduce.5.cloned.1.call-update) | async-done | bytes 8388624 | tf_op jit(solution)/shard_map/psum | solution.py:73
  386.6 9.1 %fusion.4 = (f32[2048]{0:T(1024)S(1)}, f32[2048]{0:T(1024)S(1)}) fusion(bf16[2048,2048]{1,0:T(8,128)(2,1)} %all-reduce.5.cloned.1.call-done, f32[2048]{0:T(1024)S(1)} %copy-done.13, f32[2048]{0:T(1024)S(1)} %copy-done.19, f32[2048]{0:T(1024)S(1)} %copy-done.17, bf16[2048,2048]{1,0:T(8,128)(2,1)} %param.14), kind=kLoop, calls=%fused_computation.10 | loop fusion | flops 33550336 | bytes 16818176 | tf_op jit(solution)/shard_map/reduce_sum | solution.py:15
  395.8 13.8 %add_convert_fusion = bf16[2048,2048]{1,0:T(8,128)(2,1)} fusion(f32[2048,2048]{1,0:T(8,128)} %copy-done.2, bf16[2048,2048]{1,0:T(8,128)(2,1)S(1)} %copy-done.5, bf16[2048,2048]{1,0:T(8,128)(2,1)} %param.14, f32[2048]{0:T(1024)S(1)} %broadcast_multiply_fusion, f32[2048]{0:T(1024)S(1)} %broadcast_multiply_fusion.1, f32[2048]{0:T(1024)S(1)} %copy-done.13, ...), kind=kLoop, calls=%fused_computation.7 | loop fusion | flops 46137344 | bytes 41984000 | tf_op jit(solution)/shard_map/convert_element_type | solution.py:74
  (87 shorter events, 2.6 us)
Async XLA Ops:
  7.2 6.4 %copy-start = (bf16[2048,512]{1,0:T(8,128)(2,1)S(1)}, bf16[2048,512]{1,0:T(8,128)(2,1)}, u32[]{:S(2)}) copy-start(bf16[2048,512]{1,0:T(8,128)(2,1)} %param.24) | copy-start | bytes 6291460
  7.2 180.4 %all-reduce.3.cloned.1.call-start = ((), (), s32[]{:S(2)}) async-start(), calls=%async_computation | async-start | bytes 16777216 | tf_op jit(solution)/shard_map/psum | solution.py:61
  13.6 4.7 %copy-start.7 = (bf16[2048,2048]{1,0:T(8,128)(2,1)}, bf16[2048,2048]{1,0:T(8,128)(2,1)S(1)}, u32[]{:S(2)}) copy-start(bf16[2048,2048]{1,0:T(8,128)(2,1)S(1)} %multiply_convert_fusion.1) | copy-start | bytes 25165828
  13.6 4.7 %copy-start.22 = (bf16[2048,512]{1,0:T(8,128)(2,1)S(1)}, bf16[2048,512]{1,0:T(8,128)(2,1)}, u32[]{:S(2)}) copy-start(bf16[2048,512]{1,0:T(8,128)(2,1)} %param.25) | copy-start | bytes 6291460
  13.6 9.5 %slice-start.4 = ((s8[8388608]{0:T(1024)(128)(4,1)}), s8[4194304]{0:T(1024)(128)(4,1)S(1)}, s32[]{:S(2)}) async-start(s8[8388608]{0:T(1024)(128)(4,1)} %bitcast.128), calls=%async_computation.6 | async-start | bytes 8388608
  18.4 9.8 %copy-start.25 = (bf16[2048,512]{1,0:T(8,128)(2,1)}, bf16[2048,512]{1,0:T(8,128)(2,1)S(1)}, u32[]{:S(2)}) copy-start(bf16[2048,512]{1,0:T(8,128)(2,1)S(1)} %convolution_convert_fusion.4) | copy-start | bytes 6291460
  18.4 4.8 %slice-start.5 = ((s8[8388608]{0:T(1024)(128)(4,1)}), s8[4194304]{0:T(1024)(128)(4,1)S(1)}, s32[]{:S(2)}) async-start(s8[8388608]{0:T(1024)(128)(4,1)} %bitcast.128), calls=%async_computation.7 | async-start | bytes 8388608
  18.4 4.8 %copy-start.21 = (bf16[512,2048]{1,0:T(8,128)(2,1)S(1)}, bf16[512,2048]{1,0:T(8,128)(2,1)}, u32[]{:S(2)}) copy-start(bf16[512,2048]{1,0:T(8,128)(2,1)} %param.26) | copy-start | bytes 6291460
  23.2 5.1 %copy-start.29 = (bf16[2048,512]{1,0:T(8,128)(2,1)}, bf16[2048,512]{1,0:T(8,128)(2,1)S(1)}, u32[]{:S(2)}) copy-start(bf16[2048,512]{1,0:T(8,128)(2,1)S(1)} %convolution_convert_fusion.5) | copy-start | bytes 6291460
  55.9 330.7 %all-reduce.5.cloned.1.call-start = ((), (), s32[]{:S(2)}) async-start(), calls=%async_computation.1 | async-start | bytes 16777216 | tf_op jit(solution)/shard_map/psum | solution.py:73
  56.6 5.6 %copy-start.12 = (f32[2048]{0:T(1024)}, f32[2048]{0:T(1024)S(1)}, u32[]{:S(2)}) copy-start(f32[2048]{0:T(1024)S(1)} %convert_element_type.132) | copy-start | bytes 24580
  56.6 5.6 %copy-start.23 = (bf16[2048,384]{1,0:T(8,128)(2,1)S(1)}, bf16[2048,384]{1,0:T(8,128)(2,1)}, u32[]{:S(2)}) copy-start(bf16[2048,384]{1,0:T(8,128)(2,1)} %param.22) | copy-start | bytes 4718596
  62.2 17.0 %slice-start.6 = ((s8[8388608]{0:T(1024)(128)(4,1)}), s8[4194304]{0:T(1024)(128)(4,1)S(1)}, s32[]{:S(2)}) async-start(s8[8388608]{0:T(1024)(128)(4,1)} %bitcast.130), calls=%async_computation.8 | async-start | bytes 8388608
  66.4 178.2 %copy-start.10 = (bf16[2048,384]{0,1:T(8,128)(2,1)}, bf16[2048,384]{0,1:T(8,128)(2,1)S(1)}, u32[]{:S(2)}) copy-start(bf16[2048,384]{0,1:T(8,128)(2,1)S(1)} %convolution_convert_fusion.8) | copy-start | bytes 4718596
  66.4 12.8 %slice-start.7 = ((s8[8388608]{0:T(1024)(128)(4,1)}), s8[4194304]{0:T(1024)(128)(4,1)S(1)}, s32[]{:S(2)}) async-start(s8[8388608]{0:T(1024)(128)(4,1)} %bitcast.130), calls=%async_computation.9 | async-start | bytes 8388608
  68.8 5.7 %copy-start.3 = (f32[2048,2048]{1,0:T(8,128)}, f32[2048,2048]{1,0:T(8,128)S(1)}, u32[]{:S(2)}) copy-start(f32[2048,2048]{1,0:T(8,128)S(1)} %get-tuple-element.11) | copy-start | bytes 50331652
  74.6 4.7 %copy-start.30 = (bf16[2048,512]{1,0:T(8,128)(2,1)S(1)}, bf16[2048,512]{1,0:T(8,128)(2,1)}, u32[]{:S(2)}) copy-start(bf16[2048,512]{1,0:T(8,128)(2,1)} %copy-done.29) | copy-start | bytes 6291460
  86.2 101.4 %copy-start.14 = (f32[2048]{0:T(1024)S(1)}, f32[2048]{0:T(1024)}, u32[]{:S(2)}) copy-start(f32[2048]{0:T(1024)} %param.18) | copy-start | bytes 24580
  86.2 101.4 %copy-start.15 = (f32[2048]{0:T(1024)S(1)}, f32[2048]{0:T(1024)}, u32[]{:S(2)}) copy-start(f32[2048]{0:T(1024)} %param.19) | copy-start | bytes 24580
  187.6 9.2 %copy-start.4 = (bf16[2048,2048]{1,0:T(8,128)(2,1)S(1)}, bf16[2048,2048]{1,0:T(8,128)(2,1)}, u32[]{:S(2)}) copy-start(bf16[2048,2048]{1,0:T(8,128)(2,1)} %all-reduce.3.cloned.1.call-done) | copy-start | bytes 25165828
  196.8 10.3 %copy-start.11 = (bf16[1,128,2048]{2,1,0:T(8,128)(2,1)S(1)}, bf16[1,128,2048]{2,1,0:T(8,128)(2,1)}, u32[]{:S(2)}) copy-start(bf16[1,128,2048]{2,1,0:T(8,128)(2,1)} %param.23) | copy-start | bytes 1572868
  207.2 5.7 %copy-start.2 = (f32[2048,2048]{1,0:T(8,128)}, f32[2048,2048]{1,0:T(8,128)S(1)}, u32[]{:S(2)}) copy-start(f32[2048,2048]{1,0:T(8,128)S(1)} %multiply_add_fusion) | copy-start | bytes 50331652
  212.9 22.2 %slice-start = ((s8[16777216]{0:T(1024)(128)(4,1)}), s8[4194304]{0:T(1024)(128)(4,1)S(1)}, s32[]{:S(2)}) async-start(s8[16777216]{0:T(1024)(128)(4,1)} %bitcast.126), calls=%async_computation.2 | async-start | bytes 8388608
  212.9 22.2 %slice-start.1 = ((s8[16777216]{0:T(1024)(128)(4,1)}), s8[4194304]{0:T(1024)(128)(4,1)S(1)}, s32[]{:S(2)}) async-start(s8[16777216]{0:T(1024)(128)(4,1)} %bitcast.126), calls=%async_computation.3 | async-start | bytes 8388608
  222.3 12.8 %slice-start.2 = ((s8[16777216]{0:T(1024)(128)(4,1)}), s8[4194304]{0:T(1024)(128)(4,1)S(1)}, s32[]{:S(2)}) async-start(s8[16777216]{0:T(1024)(128)(4,1)} %bitcast.126), calls=%async_computation.4 | async-start | bytes 8388608
  222.3 12.8 %slice-start.3 = ((s8[16777216]{0:T(1024)(128)(4,1)}), s8[4194304]{0:T(1024)(128)(4,1)S(1)}, s32[]{:S(2)}) async-start(s8[16777216]{0:T(1024)(128)(4,1)} %bitcast.126), calls=%async_computation.5 | async-start | bytes 8388608
  258.5 11.2 %copy-start.9 = (bf16[2048,1,3,128]{0,3,2,1:T(8,128)(2,1)S(1)}, bf16[2048,1,3,128]{0,3,2,1:T(8,128)(2,1)}, u32[]{:S(2)}) copy-start(bf16[2048,1,3,128]{0,3,2,1:T(8,128)(2,1)} %copy-done.8) | copy-start | bytes 4718596
  278.8 107.8 %copy-start.13 = (f32[2048]{0:T(1024)S(1)}, f32[2048]{0:T(1024)}, u32[]{:S(2)}) copy-start(f32[2048]{0:T(1024)} %copy-done.12) | copy-start | bytes 24580
  278.8 107.8 %copy-start.17 = (f32[2048]{0:T(1024)S(1)}, f32[2048]{0:T(1024)}, u32[]{:S(2)}) copy-start(f32[2048]{0:T(1024)} %param.16) | copy-start | bytes 24580
  278.8 107.8 %copy-start.19 = (f32[2048]{0:T(1024)S(1)}, f32[2048]{0:T(1024)}, u32[]{:S(2)}) copy-start(f32[2048]{0:T(1024)} %param.17) | copy-start | bytes 24580
  386.6 9.2 %copy-start.5 = (bf16[2048,2048]{1,0:T(8,128)(2,1)S(1)}, bf16[2048,2048]{1,0:T(8,128)(2,1)}, u32[]{:S(2)}) copy-start(bf16[2048,2048]{1,0:T(8,128)(2,1)} %all-reduce.5.cloned.1.call-done) | copy-start | bytes 25165828
  395.8 13.9 %copy-start.1 = (bf16[2048,512]{1,0:T(8,128)(2,1)S(1)}, bf16[2048,512]{1,0:T(8,128)(2,1)}, u32[]{:S(2)}) copy-start(bf16[2048,512]{1,0:T(8,128)(2,1)} %param.24) | copy-start | bytes 6291460
  (9 other events, 22.1 us)
Sparse Core Ops, SparseCore 0:
  56.0 131.5 all-reduce.2
  258.7 127.9 all-reduce.4
where the time goes:
time: 425 us; the launch traced here: 417 us
  waiting for transfers between devices  187 us (44%)
  matrix products  133 us (31%)
  other arithmetic  68.8 us (16%)
  between operations  15 us (4%)
  local copies, waits for them, and re-layouts  12.8 us (3%)
    psum x1, waiting for transfers between devices, device_step(): d_norm_h = lax.psum(part_h.astype(jnp.bfloat16), 'tp').astype(jnp.float32)  94.3 us
    psum x1, waiting for transfers between devices, device_step(): d_norm_x = lax.psum(part_x.astype(jnp.bfloat16), 'tp').astype(jnp.float32)  92.6 us
    reduce_sum x2, other arithmetic, norm_backward(): mean_grad = jnp.mean(scaled, axis=-1, keepdims=True)  18.3 us
    dot_general x1, matrix products, device_step(): jnp.einsum('tf,df->td', d_up, w_up, preferred_element_type=jnp.float32)  16.1 us
    dot_general x1, matrix products, device_step(): jnp.einsum('thz,te->hze', outputs.reshape(tokens, heads_local, head_dim),...  15.2 us
    convert_element_type x1, other arithmetic, device_step(): (d_mid + norm_backward(d_norm_x, x_in, mean_x, rstd_x, gain_x)).astype(jn...  13.8 us
    unnamed x78, local copies, waits for them, and re-layouts  12.8 us
    dot_general x1, matrix products, local_attention(): jnp.einsum('tkgd,skd->kgts', d_heads, value_rows, preferred_element_type=...  12.8 us
  transfers between devices with their start and end apart: 2, of which 2 were waited for; matrix products, arithmetic and copies ran while one was open for 16% of the time, Pallas kernels for 0%

commit v1 on v0

v1 whole, which is shorter than its diff:
```python
import functools

import jax
import jax.numpy as jnp
from jax import lax
from jax.experimental import pallas as pl
from jax.experimental.pallas import tpu as pltpu
from jax.sharding import PartitionSpec as P

MESH = pl.DeviceIdType.MESH
F32, BF16 = jnp.float32, jnp.bfloat16
NN = (((1,), (0,)), ((), ()))
NT = (((1,), (1,)), ((), ()))
TN = (((0,), (0,)), ((), ()))
SUB = 4
VMEM_BYTES = 67043328


def mm(lhs, rhs, dims=NN):
    return lax.dot_general(lhs, rhs, dims, preferred_element_type=F32)


class Ring:
    def __init__(self, size, tokens):
        me = lax.axis_index("tp")
        self.chips = size // 2
        self.chip, self.core = lax.div(me, 2), lax.rem(me, 2)
        self.way = 1 - 2 * self.core
        self.half, self.rb = tokens // 2, tokens // size
        self.sb = self.rb // SUB
        self.nxt = 2 * lax.rem(self.chip + self.way + self.chips, self.chips) + self.core
        self.prv = 2 * lax.rem(self.chip - self.way + self.chips, self.chips) + self.core
        self.peer = 2 * self.chip + 1 - self.core

    def barrier(self):
        sem = pltpu.get_barrier_semaphore()
        for other in (self.nxt, self.prv, self.peer):
            pl.semaphore_signal(sem, inc=1, device_id={"tp": other}, device_id_type=MESH)
        pl.semaphore_wait(sem, 3)

    def low(self, off):
        return pl.multiple_of(lax.rem(self.chip - off + 2 * self.chips, self.chips) * self.rb, self.rb)

    def high(self, off):
        return pl.multiple_of(self.half + lax.rem(self.chip + off, self.chips) * self.rb, self.rb)

    def mine(self, off, j):
        block = lax.rem(self.chip - self.way * off + 2 * self.chips, self.chips)
        return pl.ds(pl.multiple_of(self.core * self.half + block * self.rb + j * self.sb, self.sb), self.sb)

    def theirs(self, off, j):
        block = lax.rem(self.chip + self.way * off + 2 * self.chips, self.chips)
        return pl.ds(pl.multiple_of((1 - self.core) * self.half + block * self.rb + j * self.sb, self.sb), self.sb)

    def sub(self, j):
        return pl.ds(j * self.sb, self.sb)

    def own_sub(self, j):
        return pl.ds(pl.multiple_of(self.core * self.rb + j * self.sb, self.sb), self.sb)


class Scatter:
    def __init__(self, ring, part, dbuf, pbuf, sbuf, rbuf, dsend, drecv, rsend, rrecv):
        self.ring, self.part, self.dbuf, self.pbuf, self.sbuf, self.rbuf = ring, part, dbuf, pbuf, sbuf, rbuf
        self.dsend, self.drecv, self.rsend, self.rrecv = dsend, drecv, rsend, rrecv

    def pair(self, s):
        return pltpu.make_async_remote_copy(
            src_ref=self.dbuf.at[s], dst_ref=self.pbuf.at[s], send_sem=self.dsend.at[s], recv_sem=self.drecv.at[s],
            device_id={"tp": self.ring.peer}, device_id_type=MESH)

    def hop(self, s, j):
        rows = self.ring.sub(j)
        return pltpu.make_async_remote_copy(
            src_ref=self.sbuf.at[s, rows], dst_ref=self.rbuf.at[s, rows], send_sem=self.rsend.at[s, j], recv_sem=self.rrecv.at[s, j],
            device_id={"tp": self.ring.nxt}, device_id_type=MESH)

    def give(self, s):
        ring = self.ring
        slot = lax.rem(s, 2)
        rows = pl.ds(pl.multiple_of((1 - ring.core) * ring.rb, ring.rb), ring.rb)
        self.dbuf[s] = self.part[slot, rows, :].astype(BF16)
        self.pair(s).start()

    def combine(self, s, j, final):
        ring = self.ring
        slot = lax.rem(s, 2)
        rows = ring.sub(j)
        if j == 0:
            self.pair(s).wait_recv()
        last = ring.chips - 1

        @pl.when(s == 0)
        def _():
            total = self.part[slot, ring.own_sub(j), :] + self.pbuf[s, rows, :].astype(F32)
            self.sbuf[s, rows, :] = total.astype(BF16)
            self.hop(s, j).start()

        @pl.when(jnp.logical_and(s > 0, s < last))
        def _():
            self.hop(s - 1, j).wait_recv()
            total = self.part[slot, ring.own_sub(j), :] + self.pbuf[s, rows, :].astype(F32) + self.rbuf[s - 1, rows, :].astype(F32)
            self.sbuf[s, rows, :] = total.astype(BF16)
            self.hop(s, j).start()

        @pl.when(s == last)
        def _():
            self.hop(s - 1, j).wait_recv()
            total = self.part[slot, ring.own_sub(j), :] + self.pbuf[s, rows, :].astype(F32) + self.rbuf[s - 1, rows, :].astype(F32)
            final(j, total)

    def drain(self):
        def body(s, _):
            self.pair(s).wait_send()

            @pl.when(s < self.ring.chips - 1)
            def _():
                for j in range(SUB):
                    self.hop(s, j).wait_send()
            return 0
        lax.fori_loop(0, self.ring.chips, body, 0)


class Gather:
    def __init__(self, ring, full, asend, arecv, csend, crecv):
        self.ring, self.full = ring, full
        self.asend, self.arecv, self.csend, self.crecv = asend, arecv, csend, crecv

    def hop(self, s, j):
        rows = self.ring.mine(s, j)
        return pltpu.make_async_remote_copy(
            src_ref=self.full.at[rows], dst_ref=self.full.at[rows], send_sem=self.asend.at[s, j], recv_sem=self.arecv.at[s, j],
            device_id={"tp": self.ring.nxt}, device_id_type=MESH)

    def arrival(self, s, j):
        rows = self.ring.mine(s, j)
        return pltpu.make_async_remote_copy(
            src_ref=self.full.at[rows], dst_ref=self.full.at[rows], send_sem=self.asend.at[s - 1, j], recv_sem=self.arecv.at[s - 1, j],
            device_id={"tp": self.ring.nxt}, device_id_type=MESH)

    def across(self, s, j):
        rows = self.ring.mine(s, j)
        return pltpu.make_async_remote_copy(
            src_ref=self.full.at[rows], dst_ref=self.full.at[rows], send_sem=self.csend.at[s, j], recv_sem=self.crecv.at[s, j],
            device_id={"tp": self.ring.peer}, device_id_type=MESH)

    def from_peer(self, s, j):
        rows = self.ring.theirs(s, j)
        return pltpu.make_async_remote_copy(
            src_ref=self.full.at[rows], dst_ref=self.full.at[rows], send_sem=self.csend.at[s, j], recv_sem=self.crecv.at[s, j],
            device_id={"tp": self.ring.peer}, device_id_type=MESH)

    def begin(self, j):
        self.hop(0, j).start()
        self.across(0, j).start()

    def event(self, s, j):
        self.arrival(s, j).wait_recv()

        @pl.when(s < self.ring.chips - 1)
        def _():
            self.hop(s, j).start()
        self.across(s, j).start()

    def settle(self, s):
        for j in range(SUB):
            self.from_peer(s, j).wait_recv()

    def drain(self):
        def body(s, _):
            for j in range(SUB):
                self.across(s, j).wait_send()

            @pl.when(s < self.ring.chips - 1)
            def _():
                for j in range(SUB):
                    self.hop(s, j).wait_send()
            return 0
        lax.fori_loop(0, self.ring.chips, body, 0)


def norm_back(total, src, mean, rstd, gain):
    centred = (src.astype(F32) - mean) * rstd
    scaled = total * gain
    mean_grad = jnp.mean(scaled, axis=-1, keepdims=True)
    mean_proj = jnp.mean(scaled * centred, axis=-1, keepdims=True)
    return rstd * (scaled - mean_grad - centred * mean_proj)


def first_kernel(size, stats, gains, h_hbm, d_hbm, x_hbm, wg_hbm, wu_hbm, wd_hbm, wqkv_hbm, wout_hbm,
                 hid_hbm, dgu_hbm, dqkv_hbm, dwout_hbm, dmid_hbm,
                 wgu, wd, wqkv, wout, hin, din, xin, nrm, gu, dgu, hid, qkv, dqkv, dmid,
                 part, dbuf, pbuf, sbuf, rbuf, full, score, dprob, prob_b, ds_b, k_t, v_t, dk, dv, dwo, dwo_b, q_s, do_s, vec,
                 wsem, insem, outsem, endsem, dsend, drecv, rsend, rrecv, asend, arecv, csend, crecv):
    tokens, depth = h_hbm.shape
    ff = wd_hbm.shape[0]
    head = wout_hbm.shape[0]
    ring = Ring(size, tokens)
    rb, chips = ring.rb, ring.chips
    scatter = Scatter(ring, part, dbuf, pbuf, sbuf, rbuf, dsend, drecv, rsend, rrecv)
    gather = Gather(ring, full, asend, arecv, csend, crecv)
    scale = head ** -0.5

    weights = [pltpu.make_async_copy(wg_hbm, wgu.at[:, pl.ds(0, ff)], wsem.at[0]),
               pltpu.make_async_copy(wu_hbm, wgu.at[:, pl.ds(ff, ff)], wsem.at[1]),
               pltpu.make_async_copy(wd_hbm, wd, wsem.at[2]),
               pltpu.make_async_copy(wqkv_hbm, wqkv, wsem.at[3]),
               pltpu.make_async_copy(wout_hbm, wout, wsem.at[4])]

    def row_loads(t):
        slot = lax.rem(t, 2)
        out = []
        for k, (src, dst) in enumerate(((h_hbm, hin), (d_hbm, din), (x_hbm, xin))):
            for part_no, base in enumerate((ring.low(t + 1), ring.high(t + 1))):
                out.append(pltpu.make_async_copy(src.at[pl.ds(base, rb)], dst.at[slot, pl.ds(part_no * rb, rb)], insem.at[slot, 2 * k + part_no]))
        return out

    def row_stores(t):
        slot = lax.rem(t, 2)
        out = []
        for k, (src, dst) in enumerate(((hid, hid_hbm), (dgu, dgu_hbm))):
            for part_no, base in enumerate((ring.low(t + 1), ring.high(t + 1))):
                out.append(pltpu.make_async_copy(src.at[slot, pl.ds(part_no * rb, rb)], dst.at[pl.ds(base, rb)], outsem.at[slot, 2 * k + part_no]))
        return out

    for copy in row_loads(0):
        copy.start()
    for copy in weights:
        copy.start()
    for copy in row_loads(1):
        copy.start()
    ring.barrier()

    def normed(src, slot, t, col, gain_row):
        for part_no, base in enumerate((ring.low(t + 1), ring.high(t + 1))):
            rows = pl.ds(part_no * rb, rb)
            st = stats[pl.ds(base, rb), :]
            val = (src[slot, rows, :].astype(F32) - st[:, col:col + 1]) * st[:, col + 1:col + 2]
            nrm[rows, :] = (val * gains[gain_row:gain_row + 1, :]).astype(BF16)

    def piece(j, t):
        slot = lax.rem(t, 2)
        if j == 0:
            for copy in row_loads(t):
                copy.wait()
            normed(hin, slot, t, 2, 0)

            @pl.when(t == 0)
            def _():
                weights[0].wait()
                weights[1].wait()
            gu[...] = mm(nrm[...], wgu[...]).astype(BF16)
        elif j == 1:
            @pl.when(t == 0)
            def _():
                weights[2].wait()

            @pl.when(t >= 2)
            def _():
                for copy in row_stores(t - 2):
                    copy.wait()
            d_hidden = mm(din[slot], wd[...], NT).astype(BF16).astype(F32)
            gate_f = gu[:, :ff].astype(F32)
            up_f = gu[:, ff:].astype(F32)
            sig = 1.0 / (1.0 + jnp.exp(-gate_f))
            act = gate_f * sig
            hid[slot] = (act * up_f).astype(BF16)
            dgu[slot, :, :ff] = (d_hidden * up_f * sig * (1.0 + gate_f * (1.0 - sig))).astype(BF16)
            dgu[slot, :, ff:] = (d_hidden * act).astype(BF16)
            for copy in row_stores(t):
                copy.start()
        elif j == 2:
            part[slot] = mm(dgu[slot], wgu[...], NT)
            scatter.give(t)
        else:
            @pl.when(t == 0)
            def _():
                weights[3].wait()
            normed(xin, slot, t, 0, 1)
            val = mm(nrm[...], wqkv[...]).astype(BF16)
            qkv[pl.ds(ring.low(t + 1), rb), :] = val[:rb]
            qkv[pl.ds(ring.high(t + 1), rb), :] = val[rb:]

            @pl.when(t + 2 < chips)
            def _():
                for copy in row_loads(t + 2):
                    copy.start()

    def final(j, total):
        rows = ring.own_sub(j)
        slot = (chips - 1) % 2
        st = stats[ring.mine(0, j), :]
        d_mid = din[slot, rows, :].astype(F32) + norm_back(total, hin[slot, rows, :], st[:, 2:3], st[:, 3:4], gains[0:1, :])
        dmid[ring.sub(j), :] = d_mid
        full[ring.mine(0, j), :] = d_mid.astype(BF16)
        gather.begin(j)

    def rs_body(it, _):
        for j in range(SUB):
            @pl.when(it < chips)
            def _():
                piece(j, it)

            @pl.when(it >= 1)
            def _():
                scatter.combine(it - 1, j, final)
        return 0

    lax.fori_loop(0, chips + 1, rs_body, 0)

    tail = pltpu.make_async_copy(dmid, dmid_hbm, endsem.at[0])
    tail.start()
    k_t[...] = qkv[:, head:2 * head].T
    v_t[...] = qkv[:, 2 * head:3 * head].T
    dk[...] = jnp.zeros_like(dk)
    dv[...] = jnp.zeros_like(dv)
    dwo[...] = jnp.zeros_like(dwo)
    weights[4].wait()

    kc = min(256, tokens)
    hb = xin.at[0]

    def consume(j, s):
        low, high = ring.low(s), ring.high(s)
        if j == 0:
            gather.settle(s)
            hb[pl.ds(0, rb), :] = full[pl.ds(low, rb), :]
            hb[pl.ds(rb, rb), :] = full[pl.ds(high, rb), :]
            q_s[pl.ds(0, rb), :] = qkv[pl.ds(low, rb), 0:head]
            q_s[pl.ds(rb, rb), :] = qkv[pl.ds(high, rb), 0:head]
            do_s[...] = mm(hb[...], wout[...], NT).astype(BF16)
            lane = lax.broadcasted_iota(jnp.int32, (1, 2 * rb), 1)
            pos = jnp.where(lane < rb, low + lane, high - rb + lane)
            peak = jnp.full((1, 2 * rb), -3e38, F32)
            for base in range(0, tokens, kc):
                val = mm(qkv[base:base + kc, head:2 * head], q_s[...], NT)
                key = base + lax.broadcasted_iota(jnp.int32, (kc, 2 * rb), 0)
                val = jnp.where(key <= pos, val, -1e30)
                score[base:base + kc, :] = val
                peak = jnp.maximum(peak, jnp.max(val, axis=0, keepdims=True))
            vec[0:1, :] = peak
        elif j == 1:
            peak = vec[0:1, :]
            norm = jnp.zeros((1, 2 * rb), F32)
            dot = jnp.zeros((1, 2 * rb), F32)
            for base in range(0, tokens, kc):
                val = jnp.exp((score[base:base + kc, :] - peak) * scale)
                d_val = mm(qkv[base:base + kc, 2 * head:3 * head], do_s[...], NT)
                score[base:base + kc, :] = val
                dprob[base:base + kc, :] = d_val
                norm = norm + jnp.sum(val, axis=0, keepdims=True)
                dot = dot + jnp.sum(val * d_val, axis=0, keepdims=True)
            inv = 1.0 / norm
            vec[1:2, :] = inv
            vec[2:3, :] = dot * inv
        elif j == 2:
            inv, row_dot = vec[1:2, :], vec[2:3, :]
            for base in range(0, tokens, kc):
                rows = slice(base, base + kc)
                val = score[rows, :] * inv
                low_p = val.astype(BF16)
                low_d = (val * (dprob[rows, :] - row_dot) * scale).astype(BF16)
                prob_b[rows, :] = low_p
                ds_b[rows, :] = low_d
                dv[rows, :] += mm(low_p, do_s[...])
                dk[rows, :] += mm(low_d, q_s[...])
        else:
            out_t = mm(v_t[...], prob_b[...]).astype(BF16)
            dwo[...] += mm(out_t, hb[...])
            grad_q = mm(k_t[...], ds_b[...]).T.astype(BF16)
            dqkv[pl.ds(low, rb), 0:head] = grad_q[:rb]
            dqkv[pl.ds(high, rb), 0:head] = grad_q[rb:]

    def ag_body(it, _):
        for j in range(SUB):
            consume(j, it - 1)

            @pl.when(it < chips)
            def _():
                gather.event(it, j)
        return 0

    lax.fori_loop(1, chips + 1, ag_body, 0)

    dqkv[:, head:2 * head] = dk[...].astype(BF16)
    dqkv[:, 2 * head:3 * head] = dv[...].astype(BF16)
    dwo_b[...] = dwo[...].astype(BF16)
    ends = [pltpu.make_async_copy(dqkv, dqkv_hbm, endsem.at[1]), pltpu.make_async_copy(dwo_b, dwout_hbm, endsem.at[2])]
    for copy in ends:
        copy.start()
    for copy in row_stores(chips - 2) + row_stores(chips - 1):
        copy.wait()
    tail.wait()
    scatter.drain()
    gather.drain()
    for copy in ends:
        copy.wait()


def second_kernel(size, stats, gains, h_hbm, d_hbm, x_hbm, wqkv_hbm, hid_hbm, dgu_hbm, dqkv_hbm, dmid_hbm,
                  dx_hbm, dwqkv_hbm, dwg_hbm, dwu_hbm, dwd_hbm,
                  wqkv, dqkv, dmid, xown, dgu, hid, hid_t, hcol, dcol, xcol, n_t, ogate, oup, odown, oqkv,
                  part, dbuf, pbuf, sbuf, rbuf, full,
                  wsem, hsem, dsem, xsem, osem, dxsem, dsend, drecv, rsend, rrecv, asend, arecv, csend, crecv):
    tokens, depth = h_hbm.shape
    ff = hid_hbm.shape[1]
    ring = Ring(size, tokens)
    rb, chips = ring.rb, ring.chips
    blk = depth // chips
    scatter = Scatter(ring, part, dbuf, pbuf, sbuf, rbuf, dsend, drecv, rsend, rrecv)
    gather = Gather(ring, full, asend, arecv, csend, crecv)

    own = pl.ds(pl.multiple_of(ring.core * ring.half + ring.chip * rb, rb), rb)
    loads = [pltpu.make_async_copy(dqkv_hbm, dqkv, wsem.at[0]),
             pltpu.make_async_copy(wqkv_hbm, wqkv, wsem.at[1]),
             pltpu.make_async_copy(dgu_hbm, dgu, wsem.at[2]),
             pltpu.make_async_copy(hid_hbm, hid, wsem.at[3]),
             pltpu.make_async_copy(dmid_hbm, dmid, wsem.at[4]),
             pltpu.make_async_copy(x_hbm.at[own], xown, wsem.at[5])]

    def cols(t):
        return pl.ds(pl.multiple_of(t * blk, blk), blk)

    def col_load(src, dst, sem, t):
        slot = lax.rem(t, 2)
        return pltpu.make_async_copy(src.at[:, cols(t)], dst.at[slot], sem.at[slot])

    def store(src, dst, k, t):
        slot = lax.rem(t, 2)
        return pltpu.make_async_copy(src.at[slot], dst.at[cols(t)] if dst is not dwd_hbm else dst.at[:, cols(t)], osem.at[k, slot])

    stores = ((ogate, dwg_hbm, 0), (oup, dwu_hbm, 1), (odown, dwd_hbm, 2), (oqkv, dwqkv_hbm, 3))

    def emit(which, t, value):
        src, dst, k = stores[which]

        @pl.when(t >= 2)
        def _():
            store(src, dst, k, t - 2).wait()
        src[lax.rem(t, 2)] = value.astype(BF16)
        store(src, dst, k, t).start()

    for copy in loads[:4]:
        copy.start()
    col_load(h_hbm, hcol, hsem, 0).start()
    for copy in loads[4:]:
        copy.start()
    ring.barrier()

    def transposed(src, t, col, gain_row):
        val = (src[lax.rem(t, 2)].astype(F32) - stats[:, col:col + 1]) * stats[:, col + 1:col + 2]
        n_t[...] = (val * gains[gain_row:gain_row + 1, cols(t)]).astype(BF16).T

    def piece(j, t):
        slot = lax.rem(t, 2)
        if j == 0:
            @pl.when(t == 0)
            def _():
                loads[0].wait()
                loads[1].wait()
            rows = jnp.concatenate([dqkv[pl.ds(ring.low(t + 1), rb), :], dqkv[pl.ds(ring.high(t + 1), rb), :]], axis=0)
            part[slot] = mm(rows, wqkv[...], NT)
            scatter.give(t)
        elif j == 1:
            @pl.when(t + 1 < chips)
            def _():
                col_load(h_hbm, hcol, hsem, t + 1).start()
            col_load(h_hbm, hcol, hsem, t).wait()
            transposed(hcol, t, 2, 0)
        elif j == 2:
            @pl.when(t == 0)
            def _():
                loads[2].wait()
            emit(0, t, mm(n_t[...], dgu[:, :ff]))
        else:
            emit(1, t, mm(n_t[...], dgu[:, ff:]))

            @pl.when(t == 0)
            def _():
                loads[3].wait()
                hid_t[...] = hid[...].T

            @pl.when(t == chips - 1)
            def _():
                col_load(d_hbm, dcol, dsem, 0).start()
                col_load(x_hbm, xcol, xsem, 0).start()
                loads[4].wait()
                loads[5].wait()

    def final(j, total):
        st = stats[ring.mine(0, j), :]
        rows = ring.sub(j)
        grad = dmid[rows, :] + norm_back(total, xown[rows, :], st[:, 0:1], st[:, 1:2], gains[1:2, :])
        full[ring.mine(0, j), :] = grad.astype(BF16)
        gather.begin(j)

    def rs_body(it, _):
        for j in range(SUB):
            @pl.when(it < chips)
            def _():
                piece(j, it)

            @pl.when(it >= 1)
            def _():
                scatter.combine(it - 1, j, final)
        return 0

    lax.fori_loop(0, chips + 1, rs_body, 0)

    def out_rows(s):
        low, high = ring.low(s), ring.high(s)
        return [pltpu.make_async_copy(full.at[pl.ds(low, rb)], dx_hbm.at[pl.ds(low, rb)], dxsem.at[s, 0]),
                pltpu.make_async_copy(full.at[pl.ds(high, rb)], dx_hbm.at[pl.ds(high, rb)], dxsem.at[s, 1])]

    def consume(j, t):
        if j == 0:
            gather.settle(t)
            for copy in out_rows(t):
                copy.start()

            @pl.when(t + 1 < chips)
            def _():
                col_load(d_hbm, dcol, dsem, t + 1).start()
                col_load(x_hbm, xcol, xsem, t + 1).start()
            col_load(d_hbm, dcol, dsem, t).wait()
            emit(2, t, mm(hid_t[...], dcol[lax.rem(t, 2)]))
        elif j == 1:
            col_load(x_hbm, xcol, xsem, t).wait()
            transposed(xcol, t, 0, 1)
        elif j == 2:
            emit(3, t, mm(n_t[...], dqkv[...]))

    def ag_body(it, _):
        for j in range(SUB):
            consume(j, it - 1)

            @pl.when(it < chips)
            def _():
                gather.event(it, j)
        return 0

    lax.fori_loop(1, chips + 1, ag_body, 0)

    for src, dst, k in stores:
        store(src, dst, k, chips - 2).wait()
        store(src, dst, k, chips - 1).wait()
    scatter.drain()
    gather.drain()

    def finish(s, _):
        for copy in out_rows(s):
            copy.wait()
        return 0
    lax.fori_loop(0, chips, finish, 0)


def solution(mesh):
    size = mesh.shape["tp"]
    chips = size // 2

    def ring_scratch(rb, depth):
        return [pltpu.VMEM((2, 2 * rb, depth), F32), pltpu.VMEM((chips, rb, depth), BF16), pltpu.VMEM((chips, rb, depth), BF16),
                pltpu.VMEM((chips - 1, rb, depth), BF16), pltpu.VMEM((chips - 1, rb, depth), BF16)]

    def ring_sems():
        dma = pltpu.SemaphoreType.DMA
        return [dma((chips,)), dma((chips,)), dma((chips - 1, SUB)), dma((chips - 1, SUB)),
                dma((chips - 1, SUB)), dma((chips - 1, SUB)), dma((chips, SUB)), dma((chips, SUB))]

    def device_step(x_in, h_mid, mean_x, rstd_x, mean_h, rstd_h, gain_x, gain_h, w_qkv, w_out, w_gate, w_up, w_down, d_out):
        tokens, depth = x_in.shape
        head = w_out.shape[1]
        ff = w_gate.shape[1]
        width = w_qkv.shape[1]
        rb = tokens // size
        blk = depth // chips
        dma = pltpu.SemaphoreType.DMA
        stats = jnp.stack([mean_x, rstd_x, mean_h, rstd_h], axis=1)
        gains = jnp.stack([gain_h, gain_x], axis=0).astype(F32)
        any_spec = pl.BlockSpec(memory_space=pl.ANY)
        vmem_spec = pl.BlockSpec(memory_space=pltpu.VMEM)
        shape = jax.ShapeDtypeStruct

        hidden, d_gu, d_qkv, d_w_out, d_mid = pl.pallas_call(
            functools.partial(first_kernel, size),
            out_shape=(shape((tokens, ff), BF16), shape((tokens, 2 * ff), BF16), shape((tokens, width), BF16),
                       shape((head, depth), BF16), shape((rb, depth), F32)),
            in_specs=[vmem_spec] * 2 + [any_spec] * 8,
            out_specs=[any_spec] * 5,
            scratch_shapes=[
                pltpu.VMEM((depth, 2 * ff), BF16), pltpu.VMEM((ff, depth), BF16), pltpu.VMEM((depth, width), BF16), pltpu.VMEM((head, depth), BF16),
                pltpu.VMEM((2, 2 * rb, depth), BF16), pltpu.VMEM((2, 2 * rb, depth), BF16), pltpu.VMEM((2, 2 * rb, depth), BF16),
                pltpu.VMEM((2 * rb, depth), BF16), pltpu.VMEM((2 * rb, 2 * ff), BF16), pltpu.VMEM((2, 2 * rb, 2 * ff), BF16), pltpu.VMEM((2, 2 * rb, ff), BF16),
                pltpu.VMEM((tokens, width), BF16), pltpu.VMEM((tokens, width), BF16), pltpu.VMEM((rb, depth), F32),
                *ring_scratch(rb, depth), pltpu.VMEM((tokens, depth), BF16),
                pltpu.VMEM((tokens, 2 * rb), F32), pltpu.VMEM((tokens, 2 * rb), F32), pltpu.VMEM((tokens, 2 * rb), BF16), pltpu.VMEM((tokens, 2 * rb), BF16),
                pltpu.VMEM((head, tokens), BF16), pltpu.VMEM((head, tokens), BF16), pltpu.VMEM((tokens, head), F32), pltpu.VMEM((tokens, head), F32),
                pltpu.VMEM((head, depth), F32), pltpu.VMEM((head, depth), BF16), pltpu.VMEM((2 * rb, head), BF16), pltpu.VMEM((2 * rb, head), BF16), pltpu.VMEM((8, 2 * rb), F32),
                dma((5,)), dma((2, 6)), dma((2, 4)), dma((3,)), *ring_sems(),
            ],
            compiler_params=pltpu.CompilerParams(collective_id=0, has_side_effects=True, vmem_limit_bytes=VMEM_BYTES),
        )(stats, gains, h_mid, d_out, x_in, w_gate, w_up, w_down, w_qkv, w_out.reshape(head, depth))

        d_x, d_w_qkv, d_w_gate, d_w_up, d_w_down = pl.pallas_call(
            functools.partial(second_kernel, size),
            out_shape=(shape((tokens, depth), BF16), shape((depth, width), BF16), shape((depth, ff), BF16), shape((depth, ff), BF16), shape((ff, depth), BF16)),
            in_specs=[vmem_spec] * 2 + [any_spec] * 8,
            out_specs=[any_spec] * 5,
            scratch_shapes=[
                pltpu.VMEM((depth, width), BF16), pltpu.VMEM((tokens, width), BF16), pltpu.VMEM((rb, depth), F32), pltpu.VMEM((rb, depth), BF16),
                pltpu.VMEM((tokens, 2 * ff), BF16), pltpu.VMEM((tokens, ff), BF16), pltpu.VMEM((ff, tokens), BF16),
                pltpu.VMEM((2, tokens, blk), BF16), pltpu.VMEM((2, tokens, blk), BF16), pltpu.VMEM((2, tokens, blk), BF16), pltpu.VMEM((blk, tokens), BF16),
                pltpu.VMEM((2, blk, ff), BF16), pltpu.VMEM((2, blk, ff), BF16), pltpu.VMEM((2, ff, blk), BF16), pltpu.VMEM((2, blk, width), BF16),
                *ring_scratch(rb, depth), pltpu.VMEM((tokens, depth), BF16),
                dma((6,)), dma((2,)), dma((2,)), dma((2,)), dma((4, 2)), dma((chips, 2)), *ring_sems(),
            ],
            compiler_params=pltpu.CompilerParams(collective_id=1, has_side_effects=True, vmem_limit_bytes=VMEM_BYTES),
        )(stats, gains, h_mid, d_out, x_in, w_qkv, hidden, d_gu, d_qkv, d_mid)
        return d_x, d_w_qkv, d_w_out.reshape(w_out.shape), d_w_gate, d_w_up, d_w_down

    row_spec = P('dp', None)
    stat_spec = P('dp')
    col_spec = P(None, 'tp')
    in_specs = (row_spec, row_spec, stat_spec, stat_spec, stat_spec, stat_spec, P(None), P(None), col_spec, P('tp', None, None), col_spec, col_spec, P('tp', None), row_spec)
    out_specs = (row_spec, P('dp', 'tp'), P(('dp', 'tp'), None, None), P('dp', 'tp'), P('dp', 'tp'), P(('dp', 'tp'), None))
    return jax.shard_map(device_step, mesh=mesh, in_specs=in_specs, out_specs=out_specs, check_vma=False)
```

time: 425 us -> 228 us (0.54); the launches traced: 417 us -> 227 us
  Pallas kernels: 0 us -> 205 us
  waiting for transfers between devices: 187 us -> 0 us
  matrix products: 133 us -> 0 us
  other arithmetic: 68.8 us -> 1.41 us
  between operations: 15 us -> 0.67 us
  local copies, waits for them, and re-layouts: 12.8 us -> 19.6 us
    pallas_call x0 -> x2, Pallas kernels: none -> 205 us  [the longest x1 107 us: device_step(): pl.pallas_call(functools.partial(first_kernel, size), out_shape=(shape((t...]
    psum x2 -> x0, waiting for transfers between devices: 187 us -> none  [the longest x1 94.3 us: device_step(): d_norm_h = lax.psum(part_h.astype(jnp.bfloat16), 'tp').astype(jnp.float32)]
    dot_general x18 -> x0, matrix products: 133 us -> none  [the longest x1 16.1 us: device_step(): jnp.einsum('tf,df->td', d_up, w_up, preferred_element_type=jnp.float32)]
    convert_element_type x5 -> x1, other arithmetic: 25.8 us -> 0.63 us  [device_step(): gains = jnp.stack([gain_h, gain_x], axis=0).astype(F32)]
    reduce_sum x3 -> x0, other arithmetic: 22.9 us -> none  [the longest x2 18.3 us: norm_backward(): mean_grad = jnp.mean(scaled, axis=-1, keepdims=True)]
    add x1 -> x0, other arithmetic: 10.3 us -> none  [device_step(): d_out.astype(jnp.float32)]
    another operation x1, other arithmetic: 9.55 us -> 0.78 us  [device_step(): stats = jnp.stack([mean_x, rstd_x, mean_h, rstd_h], axis=1)]
    unnamed x78 -> x16, local copies, waits for them, and re-layouts: 12.8 us -> 16.9 us
  transfers between devices with their start and end apart: 2 -> 0, of which waited for: 2 -> 0; matrix products, arithmetic and copies ran while one was open for 16% -> 0% of each run, Pallas kernels for 0% -> 0%
where the time goes in v1:
time: 228 us; the launch traced here: 227 us
  Pallas kernels  205 us (90%)
  local copies, waits for them, and re-layouts  19.6 us (9%)
    pallas_call x1, Pallas kernels, device_step(): pl.pallas_call(functools.partial(first_kernel, size), out_shape=(shape((t...  107 us
    pallas_call x1, Pallas kernels, device_step(): pl.pallas_call(functools.partial(second_kernel, size), out_shape=(shape((...  98.2 us
    unnamed x16, local copies, waits for them, and re-layouts  16.9 us

profile of v1, /device:TPU:21, one launch (start us, length us, event | category | flops | bytes accessed | tf_op | source)
XLA Modules:
  0.0 227.2 jit_solution(12523179544909448051)
XLA Ops:
  0.6 0.7 stack.30
  1.3 0.7 stack.29
  2.0 0.6 maximum_convert_fusion.gains
  2.6 0.8 pad_maximum_fusion
  3.4 1.3 copy.25.stats
  4.8 107.2 %shard_map.181 = (bf16[2048,512]{1,0:T(8,128)(2,1)}, bf16[2048,1024]{1,0:T(8,128)(2,1)}, bf16[2048,384]{1,0:T(8,128)(2,1)}, bf16[128,2048]{1,0:T(8,128)(2,1)}, f32[128,2048]{1,0:T(8,128)}) custom-call(f32[2048,4]{1,0:T(8,128)} %copy.25.stats, f32[2,2048]{1,0:T(2,128)} %maximum_convert_fusion.gains, bf16[2048,2048]{1,0:T(8,128)(2,1)} %h_hbm.3, ...), custom_call_target="tpu_custom_call" | custom-call | tf_op jit(solution)/shard_map/pallas_call | solution.py:584
  112.0 98.2 %shard_map.182 = (bf16[2048,2048]{1,0:T(8,128)(2,1)}, bf16[2048,384]{1,0:T(8,128)(2,1)}, bf16[2048,512]{1,0:T(8,128)(2,1)}, bf16[2048,512]{1,0:T(8,128)(2,1)}, bf16[512,2048]{1,0:T(8,128)(2,1)}) custom-call(f32[2048,4]{1,0:T(8,128)} %copy.25.stats, f32[2,2048]{1,0:T(2,128)} %maximum_convert_fusion.gains, bf16[2048,2048]{1,0:T(8,128)(2,1)} %h_hbm.3, ...), custom_call_target="tpu_custom_call" | custom-call | tf_op jit(solution)/shard_map/pallas_call | solution.py:604
  210.2 0.0 copy-start.3
  210.2 8.6 %copy.32 = bf16[2048,2048]{1,0:T(8,128)(2,1)} copy(bf16[2048,2048]{1,0:T(8,128)(2,1)} %get-tuple-element.32) | data formatting | bytes 16777216
  218.8 0.0 copy-done.3
  218.8 0.0 copy-start.4
  218.8 0.0 copy-start.2
  218.8 1.1 copy.33
  220.0 0.2 copy-done.4
  220.2 0.8 copy.34
  221.0 0.2 copy-done.2
  221.1 0.0 copy-start.1
  221.1 1.3 copy.35
  222.5 1.0 copy-done.1
  223.5 0.0 copy-start
  223.5 1.3 copy.36
  224.8 1.0 copy-done
  225.8 1.3 copy.37
Async XLA Ops:
  210.2 8.6 %copy-start.3 = (bf16[2048,384]{1,0:T(8,128)(2,1)S(1)}, bf16[2048,384]{1,0:T(8,128)(2,1)}, u32[]{:S(2)}) copy-start(bf16[2048,384]{1,0:T(8,128)(2,1)} %get-tuple-element.33) | copy-start | bytes 4718596
  218.8 1.4 copy-start.4
  218.8 2.3 %copy-start.2 = (bf16[2048,512]{1,0:T(8,128)(2,1)S(1)}, bf16[2048,512]{1,0:T(8,128)(2,1)}, u32[]{:S(2)}) copy-start(bf16[2048,512]{1,0:T(8,128)(2,1)} %get-tuple-element.35) | copy-start | bytes 6291460
  221.1 2.3 %copy-start.1 = (bf16[2048,512]{1,0:T(8,128)(2,1)S(1)}, bf16[2048,512]{1,0:T(8,128)(2,1)}, u32[]{:S(2)}) copy-start(bf16[2048,512]{1,0:T(8,128)(2,1)} %get-tuple-element.36) | copy-start | bytes 6291460
  223.5 2.3 %copy-start = (bf16[512,2048]{1,0:T(8,128)(2,1)S(1)}, bf16[512,2048]{1,0:T(8,128)(2,1)}, u32[]{:S(2)}) copy-start(bf16[512,2048]{1,0:T(8,128)(2,1)} %get-tuple-element.37) | copy-start | bytes 6291460

commit v2 on v1

--- a/solution.py
+++ b/solution.py
@@ -14,6 +14,8 @@
 TN = (((0,), (0,)), ((), ()))
 SUB = 4
 VMEM_BYTES = 67043328
+SECOND_BYTES = 47 * 2 ** 20
+COPY_BYTES = 2 * 2 ** 20
 
 
 def mm(lhs, rhs, dims=NN):
@@ -179,6 +181,21 @@
         lax.fori_loop(0, self.ring.chips, body, 0)
 
 
+def stat_columns(sources, dest):
+    for k, src in enumerate(sources):
+        size, rb = src.shape
+        turned = src[...].T
+        for b in range(size):
+            dest[b * rb:(b + 1) * rb, k:k + 1] = turned[:, b:b + 1]
+
+
+def gain_rows(sources, dest):
+    for k, src in enumerate(sources):
+        count, lanes = src.shape
+        for b in range(count):
+            dest[k:k + 1, b * lanes:(b + 1) * lanes] = src[b:b + 1, :].astype(F32)
+
+
 def norm_back(total, src, mean, rstd, gain):
     centred = (src.astype(F32) - mean) * rstd
     scaled = total * gain
@@ -187,9 +204,9 @@
     return rstd * (scaled - mean_grad - centred * mean_proj)
 
 
-def first_kernel(size, stats, gains, h_hbm, d_hbm, x_hbm, wg_hbm, wu_hbm, wd_hbm, wqkv_hbm, wout_hbm,
+def first_kernel(size, mx, rx, mh, rh, gx_in, gh_in, h_hbm, d_hbm, x_hbm, wg_hbm, wu_hbm, wd_hbm, wqkv_hbm, wout_hbm,
                  hid_hbm, dgu_hbm, dqkv_hbm, dwout_hbm, dmid_hbm,
-                 wgu, wd, wqkv, wout, hin, din, xin, nrm, gu, dgu, hid, qkv, dqkv, dmid,
+                 stats, gains, wgu, wd, wqkv, wout, hin, din, xin, nrm, gu, dgu, hid, qkv, dqkv, dmid,
                  part, dbuf, pbuf, sbuf, rbuf, full, score, dprob, prob_b, ds_b, k_t, v_t, dk, dv, dwo, dwo_b, q_s, do_s, vec,
                  wsem, insem, outsem, endsem, dsend, drecv, rsend, rrecv, asend, arecv, csend, crecv):
     tokens, depth = h_hbm.shape
@@ -197,6 +214,7 @@
     head = wout_hbm.shape[0]
     ring = Ring(size, tokens)
     rb, chips = ring.rb, ring.chips
+    gx, gh = gains.at[0:1], gains.at[1:2]
     scatter = Scatter(ring, part, dbuf, pbuf, sbuf, rbuf, dsend, drecv, rsend, rrecv)
     gather = Gather(ring, full, asend, arecv, csend, crecv)
     scale = head ** -0.5
@@ -230,20 +248,23 @@
     for copy in row_loads(1):
         copy.start()
     ring.barrier()
-
-    def normed(src, slot, t, col, gain_row):
+    stat_columns((mx, rx, mh, rh), stats)
+    gain_rows((gx_in, gh_in), gains)
+
+    def normed(src, slot, t, col, gain_ref):
+        gain = gain_ref[...]
         for part_no, base in enumerate((ring.low(t + 1), ring.high(t + 1))):
             rows = pl.ds(part_no * rb, rb)
             st = stats[pl.ds(base, rb), :]
             val = (src[slot, rows, :].astype(F32) - st[:, col:col + 1]) * st[:, col + 1:col + 2]
-            nrm[rows, :] = (val * gains[gain_row:gain_row + 1, :]).astype(BF16)
+            nrm[rows, :] = (val * gain).astype(BF16)
 
     def piece(j, t):
         slot = lax.rem(t, 2)
         if j == 0:
             for copy in row_loads(t):
                 copy.wait()
-            normed(hin, slot, t, 2, 0)
+            normed(hin, slot, t, 2, gh)
 
             @pl.when(t == 0)
             def _():
@@ -276,7 +297,7 @@
             @pl.when(t == 0)
             def _():
                 weights[3].wait()
-            normed(xin, slot, t, 0, 1)
+            normed(xin, slot, t, 0, gx)
             val = mm(nrm[...], wqkv[...]).astype(BF16)
             qkv[pl.ds(ring.low(t + 1), rb), :] = val[:rb]
             qkv[pl.ds(ring.high(t + 1), rb), :] = val[rb:]
@@ -290,20 +311,20 @@
         rows = ring.own_sub(j)
         slot = (chips - 1) % 2
         st = stats[ring.mine(0, j), :]
-        d_mid = din[slot, rows, :].astype(F32) + norm_back(total, hin[slot, rows, :], st[:, 2:3], st[:, 3:4], gains[0:1, :])
+        d_mid = din[slot, rows, :].astype(F32) + norm_back(total, hin[slot, rows, :], st[:, 2:3], st[:, 3:4], gh[...])
         dmid[ring.sub(j), :] = d_mid
         full[ring.mine(0, j), :] = d_mid.astype(BF16)
         gather.begin(j)
 
     def rs_body(it, _):
         for j in range(SUB):
+            @pl.when(it >= 1)
+            def _():
+                scatter.combine(it - 1, j, final)
+
             @pl.when(it < chips)
             def _():
                 piece(j, it)
-
-            @pl.when(it >= 1)
-            def _():
-                scatter.combine(it - 1, j, final)
         return 0
 
     lax.fori_loop(0, chips + 1, rs_body, 0)
@@ -373,11 +394,10 @@
 
     def ag_body(it, _):
         for j in range(SUB):
+            @pl.when(it < chips)
+            def _():
+                gather.event(it, j)
             consume(j, it - 1)
-
-            @pl.when(it < chips)
-            def _():
-                gather.event(it, j)
         return 0
 
     lax.fori_loop(1, chips + 1, ag_body, 0)
@@ -397,15 +417,16 @@
         copy.wait()
 
 
-def second_kernel(size, stats, gains, h_hbm, d_hbm, x_hbm, wqkv_hbm, hid_hbm, dgu_hbm, dqkv_hbm, dmid_hbm,
-                  dx_hbm, dwqkv_hbm, dwg_hbm, dwu_hbm, dwd_hbm,
-                  wqkv, dqkv, dmid, xown, dgu, hid, hid_t, hcol, dcol, xcol, n_t, ogate, oup, odown, oqkv,
-                  part, dbuf, pbuf, sbuf, rbuf, full,
-                  wsem, hsem, dsem, xsem, osem, dxsem, dsend, drecv, rsend, rrecv, asend, arecv, csend, crecv):
+def second_kernel(size, mx, rx, mh, rh, gx_in, gh_in, h_hbm, d_hbm, x_hbm, wqkv_hbm, hid_hbm, dgu_hbm, dqkv_hbm, dmid_hbm,
+                  full, dwqkv, dwg, dwu, dwd,
+                  stats, gains, wqkv, dqkv, dmid, xown, dgu, hid, hid_t, hcol, dcol, xcol, n_t,
+                  part, dbuf, pbuf, sbuf, rbuf,
+                  wsem, hsem, dsem, xsem, dsend, drecv, rsend, rrecv, asend, arecv, csend, crecv):
     tokens, depth = h_hbm.shape
     ff = hid_hbm.shape[1]
     ring = Ring(size, tokens)
     rb, chips = ring.rb, ring.chips
+    gx, gh = gains.at[0:1], gains.at[1:2]
     blk = depth // chips
     scatter = Scatter(ring, part, dbuf, pbuf, sbuf, rbuf, dsend, drecv, rsend, rrecv)
     gather = Gather(ring, full, asend, arecv, csend, crecv)
@@ -425,133 +446,117 @@
         slot = lax.rem(t, 2)
         return pltpu.make_async_copy(src.at[:, cols(t)], dst.at[slot], sem.at[slot])
 
-    def store(src, dst, k, t):
-        slot = lax.rem(t, 2)
-        return pltpu.make_async_copy(src.at[slot], dst.at[cols(t)] if dst is not dwd_hbm else dst.at[:, cols(t)], osem.at[k, slot])
-
-    stores = ((ogate, dwg_hbm, 0), (oup, dwu_hbm, 1), (odown, dwd_hbm, 2), (oqkv, dwqkv_hbm, 3))
-
-    def emit(which, t, value):
-        src, dst, k = stores[which]
-
-        @pl.when(t >= 2)
-        def _():
-            store(src, dst, k, t - 2).wait()
-        src[lax.rem(t, 2)] = value.astype(BF16)
-        store(src, dst, k, t).start()
-
-    for copy in loads[:4]:
+    for copy in loads:
         copy.start()
     col_load(h_hbm, hcol, hsem, 0).start()
-    for copy in loads[4:]:
-        copy.start()
+    col_load(d_hbm, dcol, dsem, 0).start()
+    col_load(x_hbm, xcol, xsem, 0).start()
     ring.barrier()
-
-    def transposed(src, t, col, gain_row):
+    stat_columns((mx, rx, mh, rh), stats)
+    gain_rows((gx_in, gh_in), gains)
+
+    def transposed(src, t, col, gain_ref):
         val = (src[lax.rem(t, 2)].astype(F32) - stats[:, col:col + 1]) * stats[:, col + 1:col + 2]
-        n_t[...] = (val * gains[gain_row:gain_row + 1, cols(t)]).astype(BF16).T
-
-    def piece(j, t):
-        slot = lax.rem(t, 2)
+        n_t[...] = (val * gain_ref[:, cols(t)]).astype(BF16).T
+
+    def partial(t):
+        @pl.when(t == 0)
+        def _():
+            loads[0].wait()
+            loads[1].wait()
+        rows = jnp.concatenate([dqkv[pl.ds(ring.low(t + 1), rb), :], dqkv[pl.ds(ring.high(t + 1), rb), :]], axis=0)
+        part[lax.rem(t, 2)] = mm(rows, wqkv[...], NT)
+        scatter.give(t)
+
+    def fill_mlp(j, t):
         if j == 0:
             @pl.when(t == 0)
             def _():
-                loads[0].wait()
-                loads[1].wait()
-            rows = jnp.concatenate([dqkv[pl.ds(ring.low(t + 1), rb), :], dqkv[pl.ds(ring.high(t + 1), rb), :]], axis=0)
-            part[slot] = mm(rows, wqkv[...], NT)
-            scatter.give(t)
+                for copy in loads[2:]:
+                    copy.wait()
+
+            @pl.when(t + 1 < chips)
+            def _():
+                col_load(h_hbm, hcol, hsem, t + 1).start()
+                col_load(d_hbm, dcol, dsem, t + 1).start()
+            col_load(h_hbm, hcol, hsem, t).wait()
+            transposed(hcol, t, 2, gh)
         elif j == 1:
+            dwg[cols(t), :] = mm(n_t[...], dgu[:, :ff]).astype(BF16)
+        elif j == 2:
+            dwu[cols(t), :] = mm(n_t[...], dgu[:, ff:]).astype(BF16)
+        else:
+            @pl.when(t == 0)
+            def _():
+                hid_t[...] = hid[...].T
+            col_load(d_hbm, dcol, dsem, t).wait()
+            dwd[:, cols(t)] = mm(hid_t[...], dcol[lax.rem(t, 2)]).astype(BF16)
+
+    def fill_qkv(j, t):
+        if j == 0:
             @pl.when(t + 1 < chips)
             def _():
-                col_load(h_hbm, hcol, hsem, t + 1).start()
-            col_load(h_hbm, hcol, hsem, t).wait()
-            transposed(hcol, t, 2, 0)
-        elif j == 2:
-            @pl.when(t == 0)
-            def _():
-                loads[2].wait()
-            emit(0, t, mm(n_t[...], dgu[:, :ff]))
+                col_load(x_hbm, xcol, xsem, t + 1).start()
+            col_load(x_hbm, xcol, xsem, t).wait()
+            transposed(xcol, t, 0, gx)
         else:
-            emit(1, t, mm(n_t[...], dgu[:, ff:]))
-
-            @pl.when(t == 0)
-            def _():
-                loads[3].wait()
-                hid_t[...] = hid[...].T
-
-            @pl.when(t == chips - 1)
-            def _():
-                col_load(d_hbm, dcol, dsem, 0).start()
-                col_load(x_hbm, xcol, xsem, 0).start()
-                loads[4].wait()
-                loads[5].wait()
+            dwqkv[cols(t), :] = mm(n_t[...], dqkv[...]).astype(BF16)
 
     def final(j, total):
         st = stats[ring.mine(0, j), :]
         rows = ring.sub(j)
-        grad = dmid[rows, :] + norm_back(total, xown[rows, :], st[:, 0:1], st[:, 1:2], gains[1:2, :])
+        grad = dmid[rows, :] + norm_back(total, xown[rows, :], st[:, 0:1], st[:, 1:2], gx[...])
         full[ring.mine(0, j), :] = grad.astype(BF16)
         gather.begin(j)
 
+    partial(0)
+
     def rs_body(it, _):
         for j in range(SUB):
-            @pl.when(it < chips)
-            def _():
-                piece(j, it)
-
-            @pl.when(it >= 1)
-            def _():
-                scatter.combine(it - 1, j, final)
+            scatter.combine(it - 1, j, final)
+            if j == 0:
+                @pl.when(it < chips)
+                def _():
+                    partial(it)
+            fill_mlp(j, it - 1)
         return 0
 
-    lax.fori_loop(0, chips + 1, rs_body, 0)
-
-    def out_rows(s):
-        low, high = ring.low(s), ring.high(s)
-        return [pltpu.make_async_copy(full.at[pl.ds(low, rb)], dx_hbm.at[pl.ds(low, rb)], dxsem.at[s, 0]),
-                pltpu.make_async_copy(full.at[pl.ds(high, rb)], dx_hbm.at[pl.ds(high, rb)], dxsem.at[s, 1])]
-
-    def consume(j, t):
-        if j == 0:
-            gather.settle(t)
-            for copy in out_rows(t):
-                copy.start()
-
-            @pl.when(t + 1 < chips)
-            def _():
-                col_load(d_hbm, dcol, dsem, t + 1).start()
-                col_load(x_hbm, xcol, xsem, t + 1).start()
-            col_load(d_hbm, dcol, dsem, t).wait()
-            emit(2, t, mm(hid_t[...], dcol[lax.rem(t, 2)]))
-        elif j == 1:
-            col_load(x_hbm, xcol, xsem, t).wait()
-            transposed(xcol, t, 0, 1)
-        elif j == 2:
-            emit(3, t, mm(n_t[...], dqkv[...]))
+    lax.fori_loop(1, chips + 1, rs_body, 0)
 
     def ag_body(it, _):
         for j in range(SUB):
-            consume(j, it - 1)
-
-            @pl.when(it < chips)
-            def _():
-                gather.event(it, j)
+            gather.event(it, j)
+            if j < 2:
+                fill_qkv(j, it - 1)
+            else:
+                @pl.when(it == chips - 1)
+                def _():
+                    fill_qkv(j - 2, it)
         return 0
 
-    lax.fori_loop(1, chips + 1, ag_body, 0)
-
-    for src, dst, k in stores:
-        store(src, dst, k, chips - 2).wait()
-        store(src, dst, k, chips - 1).wait()
+    lax.fori_loop(1, chips, ag_body, 0)
+
+    def settle(s, _):
+        gather.settle(s)
+        return 0
+    lax.fori_loop(0, chips, settle, 0)
     scatter.drain()
     gather.drain()
 
-    def finish(s, _):
-        for copy in out_rows(s):
-            copy.wait()
-        return 0
-    lax.fori_loop(0, chips, finish, 0)
+
+def copy_kernel(dx, dwqkv, dwg, dwu, dwd, dwout_hbm, dx_hbm, dwqkv_hbm, dwg_hbm, dwu_hbm, dwd_hbm, dwout_out, staged, sem):
+    first = pltpu.make_async_copy(dwout_hbm, staged, sem.at[0])
+    first.start()
+    copies = []
+    for src, dst in ((dx, dx_hbm), (dwqkv, dwqkv_hbm), (dwg, dwg_hbm), (dwu, dwu_hbm), (dwd, dwd_hbm)):
+        copies.append(pltpu.make_async_copy(src, dst, sem.at[len(copies) + 1]))
+        copies[-1].start()
+    first.wait()
+    last = pltpu.make_async_copy(staged, dwout_out, sem.at[6])
+    last.start()
+    for copy in copies:
+        copy.wait()
+    last.wait()
 
 
 def solution(mesh):
@@ -575,8 +580,8 @@
         rb = tokens // size
         blk = depth // chips
         dma = pltpu.SemaphoreType.DMA
-        stats = jnp.stack([mean_x, rstd_x, mean_h, rstd_h], axis=1)
-        gains = jnp.stack([gain_h, gain_x], axis=0).astype(F32)
+        stats = [val.reshape(size, rb) for val in (mean_x, rstd_x, mean_h, rstd_h)]
+        gains = [gain_x.reshape(size, depth // size), gain_h.reshape(size, depth // size)]
         any_spec = pl.BlockSpec(memory_space=pl.ANY)
         vmem_spec = pl.BlockSpec(memory_space=pltpu.VMEM)
         shape = jax.ShapeDtypeStruct
@@ -585,10 +590,10 @@
             functools.partial(first_kernel, size),
             out_shape=(shape((tokens, ff), BF16), shape((tokens, 2 * ff), BF16), shape((tokens, width), BF16),
                        shape((head, depth), BF16), shape((rb, depth), F32)),
-            in_specs=[vmem_spec] * 2 + [any_spec] * 8,
+            in_specs=[vmem_spec] * 6 + [any_spec] * 8,
             out_specs=[any_spec] * 5,
             scratch_shapes=[
-                pltpu.VMEM((depth, 2 * ff), BF16), pltpu.VMEM((ff, depth), BF16), pltpu.VMEM((depth, width), BF16), pltpu.VMEM((head, depth), BF16),
+                pltpu.VMEM((tokens, 4), F32), pltpu.VMEM((2, depth), F32), pltpu.VMEM((depth, 2 * ff), BF16), pltpu.VMEM((ff, depth), BF16), pltpu.VMEM((depth, width), BF16), pltpu.VMEM((head, depth), BF16),
                 pltpu.VMEM((2, 2 * rb, depth), BF16), pltpu.VMEM((2, 2 * rb, depth), BF16), pltpu.VMEM((2, 2 * rb, depth), BF16),
                 pltpu.VMEM((2 * rb, depth), BF16), pltpu.VMEM((2 * rb, 2 * ff), BF16), pltpu.VMEM((2, 2 * rb, 2 * ff), BF16), pltpu.VMEM((2, 2 * rb, ff), BF16),
                 pltpu.VMEM((tokens, width), BF16), pltpu.VMEM((tokens, width), BF16), pltpu.VMEM((rb, depth), F32),
@@ -599,23 +604,33 @@
                 dma((5,)), dma((2, 6)), dma((2, 4)), dma((3,)), *ring_sems(),
             ],
             compiler_params=pltpu.CompilerParams(collective_id=0, has_side_effects=True, vmem_limit_bytes=VMEM_BYTES),
-        )(stats, gains, h_mid, d_out, x_in, w_gate, w_up, w_down, w_qkv, w_out.reshape(head, depth))
-
-        d_x, d_w_qkv, d_w_gate, d_w_up, d_w_down = pl.pallas_call(
+        )(*stats, *gains, h_mid, d_out, x_in, w_gate, w_up, w_down, w_qkv, w_out.reshape(head, depth))
+
+        late = [(tokens, depth), (depth, width), (depth, ff), (depth, ff), (ff, depth)]
+        results = pl.pallas_call(
             functools.partial(second_kernel, size),
-            out_shape=(shape((tokens, depth), BF16), shape((depth, width), BF16), shape((depth, ff), BF16), shape((depth, ff), BF16), shape((ff, depth), BF16)),
-            in_specs=[vmem_spec] * 2 + [any_spec] * 8,
-            out_specs=[any_spec] * 5,
+            out_shape=tuple(pltpu.VMEM(dims, BF16) for dims in late),
+            in_specs=[vmem_spec] * 6 + [any_spec] * 8,
+            out_specs=[vmem_spec] * 5,
             scratch_shapes=[
+                pltpu.VMEM((tokens, 4), F32), pltpu.VMEM((2, depth), F32),
                 pltpu.VMEM((depth, width), BF16), pltpu.VMEM((tokens, width), BF16), pltpu.VMEM((rb, depth), F32), pltpu.VMEM((rb, depth), BF16),
                 pltpu.VMEM((tokens, 2 * ff), BF16), pltpu.VMEM((tokens, ff), BF16), pltpu.VMEM((ff, tokens), BF16),
                 pltpu.VMEM((2, tokens, blk), BF16), pltpu.VMEM((2, tokens, blk), BF16), pltpu.VMEM((2, tokens, blk), BF16), pltpu.VMEM((blk, tokens), BF16),
-                pltpu.VMEM((2, blk, ff), BF16), pltpu.VMEM((2, blk, ff), BF16), pltpu.VMEM((2, ff, blk), BF16), pltpu.VMEM((2, blk, width), BF16),
-                *ring_scratch(rb, depth), pltpu.VMEM((tokens, depth), BF16),
-                dma((6,)), dma((2,)), dma((2,)), dma((2,)), dma((4, 2)), dma((chips, 2)), *ring_sems(),
+                *ring_scratch(rb, depth),
+                dma((6,)), dma((2,)), dma((2,)), dma((2,)), *ring_sems(),
             ],
-            compiler_params=pltpu.CompilerParams(collective_id=1, has_side_effects=True, vmem_limit_bytes=VMEM_BYTES),
-        )(stats, gains, h_mid, d_out, x_in, w_qkv, hidden, d_gu, d_qkv, d_mid)
+            compiler_params=pltpu.CompilerParams(collective_id=1, has_side_effects=True, vmem_limit_bytes=SECOND_BYTES),
+        )(*stats, *gains, h_mid, d_out, x_in, w_qkv, hidden, d_gu, d_qkv, d_mid)
+
+        d_x, d_w_qkv, d_w_gate, d_w_up, d_w_down, d_w_out = pl.pallas_call(
+            copy_kernel,
+            out_shape=tuple(shape(dims, BF16) for dims in late) + (shape((head, depth), BF16),),
+            in_specs=[vmem_spec] * 5 + [any_spec],
+            out_specs=[any_spec] * 6,
+            scratch_shapes=[pltpu.VMEM((head, depth), BF16), dma((7,))],
+            compiler_params=pltpu.CompilerParams(vmem_limit_bytes=COPY_BYTES),
+        )(*results, d_w_out)
         return d_x, d_w_qkv, d_w_out.reshape(w_out.shape), d_w_gate, d_w_up, d_w_down
 
     row_spec = P('dp', None)

time: 228 us -> 207 us (0.908)
  local copies, waits for them, and re-layouts: 19.6 us -> 0.01 us
    unnamed x16 -> x2, local copies, waits for them, and re-layouts: 16.9 us -> 0.01 us
    another operation x3 -> x0, local copies, waits for them, and re-layouts: 2.73 us -> none  [the longest x2 1.39 us: device_step(): gains = jnp.stack([gain_h, gain_x], axis=0).astype(F32)]
    pallas_call x1 -> x2, Pallas kernels: 98.2 us -> 97.4 us  [the longest x1 91.4 us: device_step(): pl.pallas_call(functools.partial(second_kernel, size), out_shape=tuple((p...]
where the time goes in v2:
time: 207 us
  Pallas kernels  206 us (100%)
    pallas_call x1, Pallas kernels, device_step(): pl.pallas_call(functools.partial(first_kernel, size), out_shape=(shape((t...  109 us
    pallas_call x1, Pallas kernels, device_step(): pl.pallas_call(functools.partial(second_kernel, size), out_shape=tuple((p...  91.4 us
    pallas_call x1, Pallas kernels, device_step(): pl.pallas_call(copy_kernel, out_shape=tuple((shape(dims, BF16) for dims i...  6.02 us

profile of v2, /device:TPU:21, one launch (start us, length us, event | category | flops | bytes accessed | tf_op | source)
XLA Modules:
  0.0 206.8 jit_solution(5452928415768976254)
XLA Ops:
  0.6 108.5 %shard_map.181 = (bf16[2048,512]{1,0:T(8,128)(2,1)}, bf16[2048,1024]{1,0:T(8,128)(2,1)}, bf16[2048,384]{1,0:T(8,128)(2,1)}, bf16[128,2048]{1,0:T(8,128)(2,1)}, f32[128,2048]{1,0:T(8,128)}) custom-call(f32[16,128]{1,0:T(8,128)} %bitcast.9, f32[16,128]{1,0:T(8,128)} %bitcast.11, f32[16,128]{1,0:T(8,128)} %bitcast.13, f32[16,128]{1,0:T(8,128)} %bitcast.15, ...), custom_call_target="tpu_custom_call" | custom-call | tf_op jit(solution)/shard_map/pallas_call | solution.py:589
  109.2 0.0 copy-start
  109.2 91.4 %shard_map.182 = (bf16[2048,2048]{1,0:T(8,128)(2,1)S(1)}, bf16[2048,384]{1,0:T(8,128)(2,1)S(1)}, bf16[2048,512]{1,0:T(8,128)(2,1)S(1)}, bf16[2048,512]{1,0:T(8,128)(2,1)S(1)}, bf16[512,2048]{1,0:T(8,128)(2,1)S(1)}) custom-call(f32[16,128]{1,0:T(8,128)} %bitcast.10, f32[16,128]{1,0:T(8,128)} %bitcast.12, f32[16,128]{1,0:T(8,128)} %bitcast.14, ...), custom_call_target="tpu_custom_call" | custom-call | tf_op jit(solution)/shard_map/pallas_call | solution.py:610
  200.6 0.0 copy-done
  200.6 6.0 %shard_map.183 = (bf16[2048,2048]{1,0:T(8,128)(2,1)}, bf16[2048,384]{1,0:T(8,128)(2,1)}, bf16[2048,512]{1,0:T(8,128)(2,1)}, bf16[2048,512]{1,0:T(8,128)(2,1)}, b...) custom-call(bf16[2048,2048]{1,0:T(8,128)(2,1)S(1)} %get-tuple-element.26.dx, ...), custom_call_target="tpu_custom_call" | custom-call | tf_op jit(solution)/shard_map/pallas_call | solution.py:626
Async XLA Ops:
  109.2 91.4 %copy-start = (bf16[128,2048]{1,0:T(8,128)(2,1)S(1)}, bf16[128,2048]{1,0:T(8,128)(2,1)}, u32[]{:S(2)}) copy-start(bf16[128,2048]{1,0:T(8,128)(2,1)} %get-tuple-element.31.dwout_hbm) | copy-start | bytes 1572868
